TPU v7x, 32 devices: a whole 2x2x4 slice. The times are simulated.
32 devices in a mesh: groups: 2 (over y), box: 4 (over z), sub: 2 (over x), rep: 2 (over core).
Axes of the slice: x: 2, y: 2, z: 4, core: 2. Of those that a mesh axis runs over, the one named last changes fastest.
Arguments:
- atom_data: float32 [16, 24, 4, 128], P(('groups', 'box', 'rep')), parts along dimension 0, may hold values from -0.8 to 64, as said below
- atom_type: int32 [16, 24, 128], P(('groups', 'box', 'rep')), parts along dimension 0, may hold values from 0 to 31
- tile_info: int32 [16, 24, 2], P(('groups', 'box', 'rep')), parts along dimension 0, may hold values from 1 to 128, as said below
- lj_repulsion: float32 [32], replicated, may hold values from 100 to 1000
- lj_dispersion: float32 [32], replicated, may hold values from 3 to 30
- send_tiles: int32 [16, 2, 8, 3], P(('groups', 'box', 'rep'), 'sub'), parts along dimension 0, may hold values from 0 to 23, as said below
- send_count: int32 [16, 2, 8], P(('groups', 'box', 'rep'), 'sub'), parts along dimension 0, may hold values from 1 to 3
- pair_slots: int32 [16, 2, 192, 2], P(('groups', 'box', 'rep'), 'sub'), parts along dimension 0, may hold values from 0 to 23, as said below
- pair_count: int32 [16, 2], P(('groups', 'box', 'rep'), 'sub'), parts along dimension 0, may hold values from 1 to 192
Outputs:
- forces: float32 [16, 24, 3, 128], P(('groups', 'box', 'rep'), 'sub'), parts along dimension 0
There are 2 independent parts, one for each index of `groups`. A program takes and returns all parts, laid end to end along the dimension named above; an argument that names none is the same for every part. Nothing has to cross between parts.
Inputs may be any that keep to these rules, and one draw needn't show every extreme that they name: `tile_info`: column 0 lies in 64 to 128, column 1 in 1 to 4. `send_tiles`: the 3 entries of a row are distinct. `pair_slots`: each slot w * 3 + c has c < send_count[w, s, h] for the device (h, s) that holds the pair. `atom_data`: rows 0 to 2 are coordinates in angstrom, row 3 the charge.
All inputs are finite; a program needn't handle non-finite values.
Results may differ from a plain program's by a relative error of at most 0.0003.
Values sent between devices are 32-bit elements; how exact they have to be, the bound alone decides.
No kernel may reach another device: no remote copies, remote signals or barrier semaphores. Data moves between devices by JAX's collectives and lax.ppermute only.
A program may use at most 64 MiB of HBM per device.

v0:
```python
import functools
import math

import jax
import jax.numpy as jnp
from jax import lax
from jax.experimental import pallas as pl
from jax.experimental.pallas import tpu as pltpu
from jax.sharding import PartitionSpec as P


COULOMB = 332.0636
SOFTENING = 9.0
CUTOFF_SQ = 144.0
EDGE = CUTOFF_SQ + SOFTENING
SCALE = EDGE / (CUTOFF_SQ * CUTOFF_SQ)
SCALE_REP = math.sqrt(12.0 * SCALE)
SCALE_DISP = math.sqrt(6.0 * SCALE)
SCALE_CHARGE = math.sqrt(COULOMB * SCALE)
SHIFT_REP = 2.0 / (3.0 * EDGE)
SHIFT_DISP = 1.0 / (3.0 * EDGE)
SHIFT_CHARGE = 3.0 / EDGE
LANES = 128
SUBLANES = 8
UNROLL = 4
PREPARE_VMEM = 16 * 1024 * 1024
PAIR_VMEM = 24 * 1024 * 1024
EXCLUDE = 256.0
FAR_GROUP = 1048576.0


def ceil_div(a, b):
    return (a + b - 1) // b


def log2_up(n):
    return max(1, (n - 1).bit_length())


def gathers_by_permute(boxes, replicas):
    return replicas == 2 and boxes in (2, 4, 8)


class Plan:
    def __init__(self, tiles, pairs, homes, capacity):
        self.tiles, self.pairs, self.homes, self.capacity = tiles, pairs, homes, capacity
        self.pair_rows = ceil_div(pairs, LANES)
        self.home_rows = ceil_div(homes, LANES)
        self.types = 4 * tiles
        self.near = self.types + tiles
        self.far = self.near + self.pair_rows
        self.sends = self.far + self.pair_rows
        self.count = self.sends + capacity * self.home_rows
        self.rows = ceil_div(self.count + 1, SUBLANES) * SUBLANES
        self.tile_bits = log2_up(tiles + 1)
        self.tile_pad = 1 << self.tile_bits
        self.home_pad = ceil_div(homes, SUBLANES) * SUBLANES


def pack_kernel(plan, *refs):
    sources, (out_ref, table, groups), targets, sem = refs[:8], refs[8:11], refs[11:19], refs[19]
    copies = [pltpu.make_async_copy(a, b, sem.at[n]) for n, (a, b) in enumerate(zip(sources, targets))]
    for copy in copies:
        copy.start()
    for copy in copies:
        copy.wait()
    atom_ref, type_ref, info_ref, send_ref, pair_ref, count_ref, rep_ref, disp_ref = targets
    lane = lax.broadcasted_iota(jnp.int32, (1, LANES), 1)
    lane4 = lax.broadcasted_iota(jnp.int32, (4, LANES), 1)
    row4 = lax.broadcasted_iota(jnp.int32, (4, LANES), 0)
    for t in range(plan.tiles):
        present = info_ref[0, t]
        block = atom_ref[t]
        charge = jnp.where(lane4 < present, block * SCALE_CHARGE, 0.0)
        out_ref[4 * t : 4 * t + 4, :] = jnp.where(row4 == 3, charge, block)
        kinds = jnp.where(lane < present, type_ref[t : t + 1, :], LANES - 1)
        out_ref[plan.types + t : plan.types + t + 1, :] = kinds.astype(jnp.float32)
    out_ref[plan.near : plan.rows, :] = jnp.zeros((plan.rows - plan.near, LANES), jnp.float32)
    for r in range(plan.pair_rows):
        width = min(LANES, plan.pairs - r * LANES)
        span = slice(r * LANES, r * LANES + width)
        out_ref[plan.near + r : plan.near + r + 1, 0:width] = pair_ref[0:1, span].astype(jnp.float32)
        out_ref[plan.far + r : plan.far + r + 1, 0:width] = pair_ref[1:2, span].astype(jnp.float32)
    for c in range(plan.capacity):
        for r in range(plan.home_rows):
            width = min(LANES, plan.homes - r * LANES)
            row = plan.sends + c * plan.home_rows + r
            span = slice(r * LANES, r * LANES + width)
            out_ref[row : row + 1, 0:width] = send_ref[c, 0:1, span].astype(jnp.float32)
    counts = jnp.full((1, LANES), count_ref[0, 0], jnp.int32)
    out_ref[plan.count : plan.count + 1, :] = counts.astype(jnp.float32)
    lane8 = lax.broadcasted_iota(jnp.int32, (SUBLANES, LANES), 1)
    all_rep = jnp.zeros((SUBLANES, LANES), jnp.float32)
    all_disp = all_rep
    for k in range(rep_ref.shape[0]):
        all_rep = jnp.where(lane8 == k, rep_ref[k] * SCALE_REP, all_rep)
        all_disp = jnp.where(lane8 == k, disp_ref[k] * SCALE_DISP, all_disp)
    table[0:SUBLANES, :] = all_rep
    table[SUBLANES : 2 * SUBLANES, :] = all_disp
    atom = lane.astype(jnp.float32) + 0.5
    for t in range(plan.tiles):
        run = jnp.full((1, LANES), info_ref[1, t], jnp.int32).astype(jnp.float32)
        groups[t : t + 1, :] = jnp.floor(atom / run)
    groups[plan.tiles : plan.tiles + 1, :] = jnp.zeros((1, LANES), jnp.float32)


def pair_forces(dx, dy, dz, charge, repulsive, attractive, keep):
    soft = dx * dx + dy * dy + (dz * dz + SOFTENING)
    root = lax.rsqrt(soft)
    inverse = root * root
    cube = inverse * inverse * inverse
    edge = jnp.maximum(jnp.minimum(EDGE - soft, keep), 0.0)
    repulsion = repulsive * cube * (inverse - SHIFT_REP)
    attract = attractive * (inverse - SHIFT_DISP)
    charges = charge * root * (inverse + SHIFT_CHARGE)
    weight = edge * ((repulsion - attract) * cube + charges)
    return weight * dx, weight * dy, weight * dz


def split(values):
    high = values.astype(jnp.bfloat16).astype(jnp.float32)
    rest = values - high
    middle = rest.astype(jnp.bfloat16).astype(jnp.float32)
    low = (rest - middle).astype(jnp.bfloat16).astype(jnp.float32)
    return high, middle, low


def prepare_kernel(plan, own_ref, table, groups, near_ops):
    tiles = plan.tiles
    row_ids = lax.broadcasted_iota(jnp.int32, (SUBLANES, LANES), 0)
    own_rep, own_disp = [], []
    for first in range(0, tiles, SUBLANES):
        kinds = own_ref[plan.types + first : plan.types + first + SUBLANES, :].astype(jnp.int32)
        own_rep.append(jnp.take_along_axis(table[0:SUBLANES, :], kinds, axis=1))
        own_disp.append(jnp.take_along_axis(table[SUBLANES : 2 * SUBLANES, :], kinds, axis=1))
    own_rep, own_disp = jnp.concatenate(own_rep, axis=0), jnp.concatenate(own_disp, axis=0)

    for tile in range(tiles + 1):
        if tile == tiles:
            near_ops[tile] = jnp.zeros(near_ops.shape[1:], jnp.bfloat16)
            continue
        group = groups[tile : tile + 1, :]
        record = jnp.concatenate(
            [
                own_ref[4 * tile : 4 * tile + 4, :],
                own_rep[tile : tile + 1, :],
                own_disp[tile : tile + 1, :],
                group,
                group * group,
            ],
            axis=0,
        )
        high, middle, low = split(record)
        zero = jnp.zeros_like(record)
        for block in range(7):
            if block < 3:
                minus = jnp.where(row_ids == block, -1.0, 0.0)
                wide = lambda v: jnp.broadcast_to(v[block : block + 1, :], zero.shape)
                ones_side = jnp.where(
                    row_ids == 0, wide(high), jnp.where(row_ids == 1, wide(middle), jnp.where(row_ids == 2, wide(low), 0.0))
                )
                sets = [minus, minus, minus, zero, zero, zero, ones_side, zero]
            elif block < 6:
                pick = lambda v: jnp.where(row_ids == block, v, 0.0)
                sets = [pick(high), pick(high), pick(high), pick(middle), pick(low), pick(middle), zero, zero]
            else:
                wide = lambda v, r: jnp.broadcast_to(v[r : r + 1, :], zero.shape)
                first = jnp.where(row_ids == 6, wide(high, 6) * -2.0, jnp.where(row_ids == 7, 1.0, 0.0))
                second = jnp.where(row_ids == 7, 1.0, 0.0)
                ones_side = jnp.where(row_ids == 0, wide(high, 7), jnp.where(row_ids == 1, wide(middle, 7), 0.0))
                sets = [first * EXCLUDE, second * EXCLUDE, zero, zero, zero, zero, ones_side * EXCLUDE, zero]
            near_ops[tile, :, block * LANES : (block + 1) * LANES] = jnp.concatenate(sets, axis=0).astype(jnp.bfloat16)


def pair_kernel(plan, blocks, sub_total, near_ops, groups, lj_table, *refs):
    payloads, rest = refs[:blocks], refs[blocks:]
    outs = rest[: 2 if sub_total == 2 else 1]
    (data, rep_rows, disp_rows, list_vm, list_sm, acc, sem) = rest[
        len(outs) : len(rest) - 2 * UNROLL
    ]
    sides, products = rest[len(rest) - 2 * UNROLL : len(rest) - UNROLL], rest[len(rest) - UNROLL :]
    homes, rows, cap, tiles = plan.homes, plan.rows, plan.capacity, plan.tiles
    replicas = lax.axis_size("rep")
    my_box, my_rep = lax.axis_index("box"), lax.axis_index("rep")
    me = my_box * replicas + my_rep
    row_ids = lax.broadcasted_iota(jnp.int32, (SUBLANES, LANES), 0)
    lane_ids = lax.broadcasted_iota(jnp.int32, (SUBLANES, LANES), 1)

    def bring(first, last):
        if blocks == 1:
            for h in range(homes):
                data[h * rows + first : h * rows + last, :] = payloads[0][h * rows + first : h * rows + last, :]
            return
        half = blocks // 2
        for n in range(blocks):
            home = (my_box ^ (n % half)) * replicas + (my_rep ^ (n // half))
            start = pl.multiple_of(home * rows, SUBLANES) + first
            data[pl.ds(start, last - first), :] = payloads[n][first:last, :]

    bring(plan.near, rows)

    table_rows = []
    for h in range(homes):
        for c in range(cap):
            row = h * rows + plan.sends + c * plan.home_rows
            table_rows.append(data[row : row + 1, :] + float(h * plan.tile_pad))
    slots = len(table_rows)
    padded = ceil_div(slots, LANES) * LANES
    table_rows.append(jnp.zeros((padded - slots, LANES), jnp.float32))
    table = jnp.concatenate(table_rows, axis=0)
    table = jnp.concatenate(
        [table[k * LANES : (k + 1) * LANES, :].T for k in range(padded // LANES)], axis=1
    )[0 : plan.home_pad, :]

    def stacked(offset):
        parts = [data[h * rows + offset : h * rows + offset + 1, :] for h in range(homes)]
        if plan.home_pad > homes:
            parts.append(jnp.zeros((plan.home_pad - homes, LANES), jnp.float32))
        return jnp.concatenate(parts, axis=0)

    counts = stacked(plan.count)
    near_slot = [stacked(plan.near + r) for r in range(plan.pair_rows)]
    far_slot = [stacked(plan.far + r) for r in range(plan.pair_rows)]
    near_tile = [jnp.zeros_like(counts) for _ in near_slot]
    far_tile = [jnp.zeros_like(counts) for _ in near_slot]
    for slot in range(slots):
        column = jnp.broadcast_to(table[:, slot : slot + 1], counts.shape)
        for r in range(plan.pair_rows):
            near_tile[r] = jnp.where(near_slot[r] == float(slot), column, near_tile[r])
            far_tile[r] = jnp.where(far_slot[r] == float(slot), column, far_tile[r])

    lane_f = lax.broadcasted_iota(jnp.int32, counts.shape, 1).astype(jnp.float32)
    mine = (me * plan.tile_pad).astype(jnp.float32)
    near_all = jnp.concatenate(near_tile, axis=0) - mine
    far_all = jnp.concatenate(far_tile, axis=0)
    same_all = jnp.concatenate(near_slot, axis=0) == jnp.concatenate(far_slot, axis=0)
    ranks = jnp.concatenate([lane_f + float(r * LANES) for r in range(plan.pair_rows)], axis=0)
    limit = jnp.concatenate([counts] * plan.pair_rows, axis=0)
    own = (near_all >= 0.0) & (near_all < float(plan.tile_pad)) & (ranks < limit)
    flags = jnp.where(own, 1.0, 0.0)
    list_rows = flags.shape[0]
    upper = lax.broadcasted_iota(jnp.int32, (LANES, LANES), 0) <= lax.broadcasted_iota(jnp.int32, (LANES, LANES), 1)
    upper = jnp.where(upper, 1.0, 0.0).astype(jnp.bfloat16)
    prefix = jnp.dot(flags.astype(jnp.bfloat16), upper, preferred_element_type=jnp.float32)
    totals = jnp.broadcast_to(jnp.sum(flags, axis=1, keepdims=True), flags.shape)
    below = lax.broadcasted_iota(jnp.int32, (list_rows, list_rows), 0) > lax.broadcasted_iota(
        jnp.int32, (list_rows, list_rows), 1
    )
    below = jnp.where(below, 1.0, 0.0).astype(jnp.bfloat16)
    before = jnp.dot(below, totals.astype(jnp.bfloat16), preferred_element_type=jnp.float32)
    places = jnp.where(own, before + prefix - 1.0, -1.0)
    pair_total = jnp.sum(flags).astype(jnp.int32)
    far_home = jnp.floor((far_all + 0.5) * (1.0 / plan.tile_pad))
    far_in_home = far_all - far_home * float(plan.tile_pad)
    same_f = jnp.where(same_all, 1.0, 0.0)
    wide_rows = lax.broadcasted_iota(jnp.int32, (LANES, LANES), 0).astype(jnp.float32)

    def list_block(block, carry):
        first = (block * LANES).astype(jnp.float32)
        digits = jnp.zeros((SUBLANES, LANES), jnp.float32)
        for r in range(list_rows):
            values = jnp.concatenate(
                [
                    near_all[r : r + 1, :],
                    far_in_home[r : r + 1, :],
                    far_home[r : r + 1, :],
                    same_f[r : r + 1, :],
                    jnp.zeros((SUBLANES - 4, LANES), jnp.float32),
                ],
                axis=0,
            )
            chosen = jnp.broadcast_to(places[r : r + 1, :] - first, (LANES, LANES)) == wide_rows
            chosen = jnp.where(chosen, 1.0, 0.0).astype(jnp.bfloat16)
            digits = digits + lax.dot_general(
                values.astype(jnp.bfloat16),
                chosen,
                (((1,), (1,)), ((), ())),
                preferred_element_type=jnp.float32,
            )
        near, tile, home, same = [digits[k : k + 1, :].astype(jnp.int32) for k in range(4)]
        near = jnp.where(lane_ids[0:1, :] + block * LANES < pair_total, near, tiles)
        code = ((home * plan.tile_pad + tile) * plan.tile_pad + near) * 2 + same
        list_vm[pl.ds(block, 1), :] = code
        return carry

    lax.fori_loop(0, (pair_total + 3 * UNROLL) // LANES + 1, list_block, 0)
    list_copy = pltpu.make_async_copy(list_vm, list_sm, sem)
    list_copy.start()

    bring(0, plan.near)
    for tile in range(tiles + 1):
        acc[tile] = jnp.zeros((3, SUBLANES, LANES), jnp.float32)

    all_rep, all_disp = lj_table[0:SUBLANES, :], lj_table[SUBLANES : 2 * SUBLANES, :]

    def look_up(h, carry):
        for first in range(0, tiles, SUBLANES):
            source = pl.ds(pl.multiple_of(h * rows + plan.types, SUBLANES) + first, SUBLANES)
            kinds = data[source, :].astype(jnp.int32)
            target = pl.ds(pl.multiple_of(h * plan.tile_pad, SUBLANES) + first, SUBLANES)
            rep_rows[target, :] = jnp.take_along_axis(all_rep, kinds, axis=1)
            disp_rows[target, :] = jnp.take_along_axis(all_disp, kinds, axis=1)
        return carry

    if homes <= 8:
        for h in range(homes):
            look_up(h, 0)
    else:
        lax.fori_loop(0, homes, look_up, 0)
    list_copy.wait()

    def decode(place):
        code = list_sm[place // LANES, place % LANES]
        near = (code >> 1) & (plan.tile_pad - 1)
        far = code >> (1 + plan.tile_bits)
        return near, far, code & 1

    ones = jnp.where(row_ids < 3, 1.0, 0.0)

    def far_side(place, target):
        near, far, same = decode(place)
        base = (far >> plan.tile_bits) * rows + (far & (plan.tile_pad - 1)) * 4
        same_row = jnp.full((1, LANES), same, jnp.int32).astype(jnp.float32)
        group = groups[pl.ds(near, 1), :] * same_row
        record = jnp.concatenate(
            [
                data[pl.ds(pl.multiple_of(base, 4), 4), :],
                rep_rows[pl.ds(far, 1), :],
                disp_rows[pl.ds(far, 1), :],
                group,
                group * group + (1.0 - same_row) * FAR_GROUP,
            ],
            axis=0,
        )
        high, middle, low = split(record)
        sides = jnp.concatenate([high, middle, low, high, high, middle, ones, jnp.zeros_like(ones)], axis=0)
        target[...] = sides.astype(jnp.bfloat16).T

    def multiply(place, side, target):
        near, _, _ = decode(place)
        target[...] = jnp.dot(side[...], near_ops[near], preferred_element_type=jnp.float32)

    def add_forces(place, terms):
        near, _, _ = decode(place)
        total = None
        for step in range(LANES // SUBLANES):
            span = slice(step * SUBLANES, (step + 1) * SUBLANES)
            parts = pair_forces(*[terms[span, k * LANES : (k + 1) * LANES] for k in range(7)])
            total = parts if total is None else [t + p for t, p in zip(total, parts)]
        for r in range(3):
            acc[near, r] += total[r]

    for k in range(UNROLL):
        far_side(k, sides[k])
    for k in range(UNROLL):
        multiply(k, sides[k], products[k])
        far_side(UNROLL + k, sides[k])

    def some_pairs(step, carry):
        place = step * UNROLL
        for k in range(UNROLL):
            add_forces(place + k, products[k])
            multiply(place + UNROLL + k, sides[k], products[k])
            far_side(place + 2 * UNROLL + k, sides[k])
        return carry

    lax.fori_loop(0, (pair_total + UNROLL - 1) // UNROLL, some_pairs, 0)

    if sub_total == 2:
        half = tiles // 2
        side = lax.axis_index("sub")
        for n in range(2):
            first = (side ^ n) * half
            for t in range(half):
                for r in range(3):
                    outs[n][3 * t + r] = jnp.sum(acc[first + t, r], axis=0, keepdims=True)
    else:
        for t in range(tiles):
            outs[0][t] = jnp.sum(acc[t], axis=1)


def per_device(
    atom_data,
    atom_type,
    tile_info,
    lj_repulsion,
    lj_dispersion,
    send_tiles,
    send_count,
    pair_slots,
    pair_count,
):
    box_total = lax.axis_size("box")
    replicas = lax.axis_size("rep")
    sub_total = lax.axis_size("sub")
    tiles = atom_data.shape[1]
    homes, capacity = send_tiles.shape[2:]
    pairs = pair_slots.shape[2]
    plan = Plan(tiles, pairs, homes, capacity)
    vmem = pl.BlockSpec(memory_space=pltpu.VMEM)
    smem = pl.BlockSpec(memory_space=pltpu.SMEM)
    hbm = pl.BlockSpec(memory_space=pltpu.HBM)
    info = tile_info[0].T
    raw = (atom_data[0], atom_type[0], info, send_tiles[0].transpose(2, 0, 1), pair_slots[0, 0].T, pair_count)
    raw += (lj_repulsion, lj_dispersion)
    places = (pltpu.VMEM, pltpu.VMEM, pltpu.SMEM, pltpu.VMEM, pltpu.VMEM, pltpu.SMEM, pltpu.SMEM, pltpu.SMEM)
    payload, lj_table, groups = pl.pallas_call(
        functools.partial(pack_kernel, plan),
        out_shape=[
            jax.ShapeDtypeStruct((plan.rows, LANES), jnp.float32),
            jax.ShapeDtypeStruct((2 * SUBLANES, LANES), jnp.float32),
            jax.ShapeDtypeStruct((tiles + 1, LANES), jnp.float32),
        ],
        in_specs=[hbm] * len(raw),
        out_specs=[vmem] * 3,
        scratch_shapes=[place(array.shape, array.dtype) for place, array in zip(places, raw)]
        + [pltpu.SemaphoreType.DMA((len(raw),))],
        name="pack",
    )(*raw)
    near_ops = pl.pallas_call(
        functools.partial(prepare_kernel, plan),
        out_shape=jax.ShapeDtypeStruct((tiles + 1, 8 * SUBLANES, 7 * LANES), jnp.bfloat16),
        in_specs=[vmem] * 3,
        out_specs=vmem,
        compiler_params=pltpu.CompilerParams(vmem_limit_bytes=PREPARE_VMEM),
        cost_estimate=pl.CostEstimate(flops=4000000, bytes_accessed=4000000, transcendentals=0),
        name="prepare",
    )(payload, lj_table, groups)
    tables = (near_ops, groups, lj_table)

    if gathers_by_permute(box_total, replicas):
        blocks = [payload]
        for k in range(1, box_total):
            blocks.append(lax.ppermute(payload, "box", [(i, i ^ k) for i in range(box_total)]))
        for k in range(box_total):
            blocks.append(lax.ppermute(blocks[k], "rep", [(0, 1), (1, 0)]))
    else:
        blocks = [lax.all_gather(payload, ("box", "rep"), axis=0, tiled=True)]

    if sub_total == 2:
        outs = [jax.ShapeDtypeStruct((tiles // 2 * 3, 1, LANES), jnp.float32)] * 2
    else:
        outs = [jax.ShapeDtypeStruct((tiles, 3, LANES), jnp.float32)]
    list_rows = ceil_div(homes * pairs + 3 * UNROLL, LANES) + 1
    results = pl.pallas_call(
        functools.partial(pair_kernel, plan, len(blocks), sub_total),
        out_shape=outs,
        in_specs=[vmem] * (3 + len(blocks)),
        out_specs=[vmem] * len(outs),
        scratch_shapes=[
            pltpu.VMEM((homes * plan.rows, LANES), jnp.float32),
            pltpu.VMEM((homes * plan.tile_pad, LANES), jnp.float32),
            pltpu.VMEM((homes * plan.tile_pad, LANES), jnp.float32),
            pltpu.VMEM((list_rows, LANES), jnp.int32),
            pltpu.SMEM((list_rows, LANES), jnp.int32),
            pltpu.VMEM((tiles + 1, 3, SUBLANES, LANES), jnp.float32),
            pltpu.SemaphoreType.DMA,
        ]
        + [pltpu.VMEM((LANES, 8 * SUBLANES), jnp.bfloat16)] * UNROLL
        + [pltpu.VMEM((LANES, 7 * LANES), jnp.float32)] * UNROLL,
        compiler_params=pltpu.CompilerParams(vmem_limit_bytes=PAIR_VMEM),
        name="pairs",
    )(*tables, *blocks)
    if sub_total == 2:
        mine, theirs = results
        arrived = lax.ppermute(theirs, "sub", [(0, 1), (1, 0)])
        return (mine + arrived).reshape(1, tiles // 2, 3, LANES)
    return lax.psum_scatter(results[0], "sub", scatter_dimension=0, tiled=True)[None]


def solution(mesh):
    placed = (
        P(("groups", "box", "rep"), None, None, None),
        P(("groups", "box", "rep"), None, None),
        P(("groups", "box", "rep"), None, None),
        P(),
        P(),
        P(("groups", "box", "rep"), "sub", None, None),
        P(("groups", "box", "rep"), "sub", None),
        P(("groups", "box", "rep"), "sub", None, None),
        P(("groups", "box", "rep"), "sub"),
    )
    return jax.shard_map(
        per_device,
        mesh=mesh,
        in_specs=placed,
        out_specs=P(("groups", "box", "rep"), "sub", None, None),
        check_vma=False,
    )
```

profile of v0, /device:TPU:5, one launch (start us, length us, event | category | flops | bytes accessed | tf_op | source)
XLA Modules:
  0.0 30.6 jit_solution(1973456655816206650)
XLA Ops:
  0.7 1.6 %pack.1 = (f32[128,128]{1,0:T(8,128)}, f32[16,128]{1,0:T(8,128)}, f32[25,128]{1,0:T(8,128)}) custom-call(f32[24,4,128]{2,1,0:T(4,128)} %bitcast.12, s32[24,128]{1,0:T(8,128)} %bitcast.13, s32[2,24]{1,0:T(2,128)} %bitcast.16, s32[3,1,8]{2,1,0:T(1,128)} %bitcast.15, s32[2,192]{1,0:T(2,128)} %bitcast.14, s32[1,1]{1,0:T(1,128)S(6)} %copy.9.refs_5_, f32[32]{0:T(128)} %refs_6_.1, ...), custom_call_target="tpu_custom_call" | custom-call | tf_op jit(solution)/shard_map/pack/pallas_call | solution.py:407
  2.3 3.4 %collective-permute-start.2 = (f32[128,128]{1,0:T(8,128)}, f32[128,128]{1,0:T(8,128)S(1)}, u32[]{:S(2)}, u32[]{:S(2)}) collective-permute-start(f32[128,128]{1,0:T(8,128)} %get-tuple-element.10.own_ref.refs_0_), channel_id=1, source_target_pairs={{0,12},{4,8},{8,4},{12,0},{1,13},{5,9},{9,5},{13,1},{2,14},{6,10},... | collective-permute-start | bytes 196616 | tf_op jit(solution)/shard_map/ppermute | solution.py:434
  5.7 0.0 collective-permute-start.1
  5.7 0.4 %collective-permute-start = (f32[128,128]{1,0:T(8,128)}, f32[128,128]{1,0:T(8,128)S(1)}, u32[]{:S(2)}, u32[]{:S(2)}) collective-permute-start(f32[128,128]{1,0:T(8,128)} %get-tuple-element.10.own_ref.refs_0_), channel_id=1, source_target_pairs={{0,4},{4,0},{8,12},{12,8},{1,5},{5,1},{9,13},{13,9},{2,6},{6,2},{1... | collective-permute-start | bytes 196616 | tf_op jit(solution)/shard_map/ppermute | solution.py:434
  6.0 1.4 %collective-permute-start.3 = (f32[128,128]{1,0:T(8,128)}, f32[128,128]{1,0:T(8,128)S(1)}, u32[]{:S(2)}, u32[]{:S(2)}) collective-permute-start(f32[128,128]{1,0:T(8,128)} %get-tuple-element.10.own_ref.refs_0_), channel_id=1, source_target_pairs={{0,1},{1,0},{2,3},{3,2},{4,5},{5,4},{6,7},{7,6},{8,9},{9,8},{10,11... | collective-permute-start | bytes 196616 | tf_op jit(solution)/shard_map/ppermute | solution.py:436
  7.4 0.2 collective-permute-done.2.refs_3_
  7.6 2.1 %collective-permute-start.6 = (f32[128,128]{1,0:T(8,128)S(1)}, f32[128,128]{1,0:T(8,128)S(1)}, u32[]{:S(2)}, u32[]{:S(2)}) collective-permute-start(f32[128,128]{1,0:T(8,128)S(1)} %collective-permute-done.2.refs_3_), channel_id=1, source_target_pairs={{0,1},{1,0},{2,3},{3,2},{4,5},{5,4},{6,7},{7,6},{8,9},{9,8},{10,11... | collective-permute-start | bytes 196616 | tf_op jit(solution)/shard_map/ppermute | solution.py:436
  9.7 2.0 %collective-permute-done.1.refs_2_ = f32[128,128]{1,0:T(8,128)S(1)} collective-permute-done((f32[128,128]{1,0:T(8,128)}, f32[128,128]{1,0:T(8,128)S(1)}, u32[]{:S(2)}, u32[]{:S(2)}) %collective-permute-start.1) | collective-permute-done | bytes 65568 | tf_op jit(solution)/shard_map/ppermute | solution.py:434
  11.7 0.7 %collective-permute-start.5 = (f32[128,128]{1,0:T(8,128)S(1)}, f32[128,128]{1,0:T(8,128)S(1)}, u32[]{:S(2)}, u32[]{:S(2)}) collective-permute-start(f32[128,128]{1,0:T(8,128)S(1)} %collective-permute-done.1.refs_2_), channel_id=1, source_target_pairs={{0,1},{1,0},{2,3},{3,2},{4,5},{5,4},{6,7},{7,6},{8,9},{9,8},{10,11... | collective-permute-start | bytes 196616 | tf_op jit(solution)/shard_map/ppermute | solution.py:436
  12.4 0.0 collective-permute-done.refs_1_
  12.4 0.0 collective-permute-start.4
  12.4 0.8 %copy-done = f32[128,128]{1,0:T(8,128)S(1)} copy-done((f32[128,128]{1,0:T(8,128)S(1)}, f32[128,128]{1,0:T(8,128)}, u32[]{:S(2)}) %copy-start) | copy-done | bytes 65560
  13.3 0.7 %copy-done.2 = f32[25,128]{1,0:T(8,128)S(1)} copy-done((f32[25,128]{1,0:T(8,128)S(1)}, f32[25,128]{1,0:T(8,128)}, u32[]{:S(2)}) %copy-start.2) | copy-done | bytes 12824
  14.0 0.7 %copy-done.4 = f32[16,128]{1,0:T(8,128)S(1)} copy-done((f32[16,128]{1,0:T(8,128)S(1)}, f32[16,128]{1,0:T(8,128)}, u32[]{:S(2)}) %copy-start.4) | copy-done | bytes 8216
  14.7 0.4 %prepare.1.near_ops = bf16[25,64,896]{2,1,0:T(8,128)(2,1)S(1)} custom-call(f32[128,128]{1,0:T(8,128)S(1)} %copy-done, f32[16,128]{1,0:T(8,128)S(1)} %copy-done.4, f32[25,128]{1,0:T(8,128)S(1)} %copy-done.2), custom_call_target="tpu_custom_call" | custom-call | flops 4000000 | bytes 4000000 | tf_op jit(solution)/shard_map/prepare/pallas_call | solution.py:420
  15.1 0.0 collective-permute-done.3.refs_4_
  15.2 0.0 collective-permute-done.6.refs_7_
  15.2 0.0 collective-permute-done.5.refs_6_
  15.2 0.0 collective-permute-done.4.refs_5_
  15.2 0.3 %copy-done.1 = f32[128,128]{1,0:T(8,128)S(1)} copy-done((f32[128,128]{1,0:T(8,128)S(1)}, f32[128,128]{1,0:T(8,128)}, u32[]{:S(2)}) %copy-start.1) | copy-done | bytes 65560
  15.5 11.8 %pairs.1 = (f32[36,1,128]{2,1,0:T(1,128)S(1)}, f32[36,1,128]{2,1,0:T(1,128)S(1)}) custom-call(bf16[25,64,896]{2,1,0:T(8,128)(2,1)S(1)} %prepare.1.near_ops, f32[25,128]{1,0:T(8,128)S(1)} %copy-done.3, f32[16,128]{1,0:T(8,128)S(1)} %copy-done.4, f32[128,128]{1,0:T(8,128)S(1)} %copy-done.1, f32[128,128]{1,0:T(8,128)S(1)} %collective-permute-done.refs_1_, ...), custom_call_target="tpu_custom_call" | custom-call | tf_op jit(solution)/shard_map/pairs/pallas_call | solution.py:445
  27.3 0.1 collective-permute-start.7
  27.4 2.6 %collective-permute-done.7 = f32[36,1,128]{2,1,0:T(1,128)S(1)} collective-permute-done((f32[36,1,128]{2,1,0:T(1,128)S(1)}, f32[36,1,128]{2,1,0:T(1,128)S(1)}, u32[]{:S(2)}, u32[]{:S(2)}) %collective-permute-start.7) | collective-permute-done | bytes 18464 | tf_op jit(solution)/shard_map/ppermute | solution.py:466
  30.0 0.6 %add.3 = f32[36,1,128]{2,1,0:T(1,128)} add(f32[36,1,128]{2,1,0:T(1,128)S(1)} %get-tuple-element.13, f32[36,1,128]{2,1,0:T(1,128)S(1)} %collective-permute-done.7) | non-fusion elementwise | flops 4608 | bytes 55296 | tf_op jit(solution)/shard_map/add | solution.py:467
  (6 shorter events, 0.0 us)
Async XLA Ops:
  2.3 5.3 %collective-permute-start.2 = (f32[128,128]{1,0:T(8,128)}, f32[128,128]{1,0:T(8,128)S(1)}, u32[]{:S(2)}, u32[]{:S(2)}) collective-permute-start(f32[128,128]{1,0:T(8,128)} %get-tuple-element.10.own_ref.refs_0_), channel_id=1, source_target_pairs={{0,12},{4,8},{8,4},{12,0},{1,13},{5,9},{9,5},{13,1},{2,14},{6,10},... | collective-permute-start | bytes 196616 | tf_op jit(solution)/shard_map/ppermute | solution.py:434
  5.7 6.0 %collective-permute-start.1 = (f32[128,128]{1,0:T(8,128)}, f32[128,128]{1,0:T(8,128)S(1)}, u32[]{:S(2)}, u32[]{:S(2)}) collective-permute-start(f32[128,128]{1,0:T(8,128)} %get-tuple-element.10.own_ref.refs_0_), channel_id=1, source_target_pairs={{0,8},{4,12},{8,0},{12,4},{1,9},{5,13},{9,1},{13,5},{2,10},{6,14},... | collective-permute-start | bytes 196616 | tf_op jit(solution)/shard_map/ppermute | solution.py:434
  5.7 6.8 %collective-permute-start = (f32[128,128]{1,0:T(8,128)}, f32[128,128]{1,0:T(8,128)S(1)}, u32[]{:S(2)}, u32[]{:S(2)}) collective-permute-start(f32[128,128]{1,0:T(8,128)} %get-tuple-element.10.own_ref.refs_0_), channel_id=1, source_target_pairs={{0,4},{4,0},{8,12},{12,8},{1,5},{5,1},{9,13},{13,9},{2,6},{6,2},{1... | collective-permute-start | bytes 196616 | tf_op jit(solution)/shard_map/ppermute | solution.py:434
  6.0 9.1 %collective-permute-start.3 = (f32[128,128]{1,0:T(8,128)}, f32[128,128]{1,0:T(8,128)S(1)}, u32[]{:S(2)}, u32[]{:S(2)}) collective-permute-start(f32[128,128]{1,0:T(8,128)} %get-tuple-element.10.own_ref.refs_0_), channel_id=1, source_target_pairs={{0,1},{1,0},{2,3},{3,2},{4,5},{5,4},{6,7},{7,6},{8,9},{9,8},{10,11... | collective-permute-start | bytes 196616 | tf_op jit(solution)/shard_map/ppermute | solution.py:436
  7.6 7.6 %collective-permute-start.6 = (f32[128,128]{1,0:T(8,128)S(1)}, f32[128,128]{1,0:T(8,128)S(1)}, u32[]{:S(2)}, u32[]{:S(2)}) collective-permute-start(f32[128,128]{1,0:T(8,128)S(1)} %collective-permute-done.2.refs_3_), channel_id=1, source_target_pairs={{0,1},{1,0},{2,3},{3,2},{4,5},{5,4},{6,7},{7,6},{8,9},{9,8},{10,11... | collective-permute-start | bytes 196616 | tf_op jit(solution)/shard_map/ppermute | solution.py:436
  11.7 3.5 %collective-permute-start.5 = (f32[128,128]{1,0:T(8,128)S(1)}, f32[128,128]{1,0:T(8,128)S(1)}, u32[]{:S(2)}, u32[]{:S(2)}) collective-permute-start(f32[128,128]{1,0:T(8,128)S(1)} %collective-permute-done.1.refs_2_), channel_id=1, source_target_pairs={{0,1},{1,0},{2,3},{3,2},{4,5},{5,4},{6,7},{7,6},{8,9},{9,8},{10,11... | collective-permute-start | bytes 196616 | tf_op jit(solution)/shard_map/ppermute | solution.py:436
  12.4 2.7 %collective-permute-start.4 = (f32[128,128]{1,0:T(8,128)S(1)}, f32[128,128]{1,0:T(8,128)S(1)}, u32[]{:S(2)}, u32[]{:S(2)}) collective-permute-start(f32[128,128]{1,0:T(8,128)S(1)} %collective-permute-done.refs_1_), channel_id=1, source_target_pairs={{0,1},{1,0},{2,3},{3,2},{4,5},{5,4},{6,7},{7,6},{8,9},{9,8},{10,11... | collective-permute-start | bytes 196616 | tf_op jit(solution)/shard_map/ppermute | solution.py:436
  12.4 0.8 %copy-start = (f32[128,128]{1,0:T(8,128)S(1)}, f32[128,128]{1,0:T(8,128)}, u32[]{:S(2)}) copy-start(f32[128,128]{1,0:T(8,128)} %get-tuple-element.10.own_ref.refs_0_) | copy-start | bytes 196612
  13.3 0.7 %copy-start.2 = (f32[25,128]{1,0:T(8,128)S(1)}, f32[25,128]{1,0:T(8,128)}, u32[]{:S(2)}) copy-start(f32[25,128]{1,0:T(8,128)} %get-tuple-element.12.groups) | copy-start | bytes 38404
  14.0 0.7 %copy-start.4 = (f32[16,128]{1,0:T(8,128)S(1)}, f32[16,128]{1,0:T(8,128)}, u32[]{:S(2)}) copy-start(f32[16,128]{1,0:T(8,128)} %get-tuple-element.11.table.lj_table) | copy-start | bytes 24580
  14.7 0.8 %copy-start.1 = (f32[128,128]{1,0:T(8,128)S(1)}, f32[128,128]{1,0:T(8,128)}, u32[]{:S(2)}) copy-start(f32[128,128]{1,0:T(8,128)} %get-tuple-element.10.own_ref.refs_0_) | copy-start | bytes 196612
  14.7 0.8 %copy-start.3 = (f32[25,128]{1,0:T(8,128)S(1)}, f32[25,128]{1,0:T(8,128)}, u32[]{:S(2)}) copy-start(f32[25,128]{1,0:T(8,128)} %get-tuple-element.12.groups) | copy-start | bytes 38404
  27.3 2.7 %collective-permute-start.7 = (f32[36,1,128]{2,1,0:T(1,128)S(1)}, f32[36,1,128]{2,1,0:T(1,128)S(1)}, u32[]{:S(2)}, u32[]{:S(2)}) collective-permute-start(f32[36,1,128]{2,1,0:T(1,128)S(1)} %get-tuple-element.14), channel_id=1, source_target_pairs={{0,2},{2,0},{1,3},{3,1},{4,6},{6,4},{5,7},{7,5},{8,10},{10,8},{9,1... | collective-permute-start | bytes 55304 | tf_op jit(solution)/shard_map/ppermute | solution.py:466
where the time goes:
time: 31 us; the launch traced here: 30.6 us
  Pallas kernels  13.8 us (45%)
  starting transfers between devices  8.08 us (26%)
  waiting for transfers between devices  4.79 us (15%)
  local copies, waits for them, and re-layouts  2.6 us (8%)
  between operations  0.73 us (2%)
  other arithmetic  0.63 us (2%)
    pallas_call x1, Pallas kernels, per_device(): pl.pallas_call(functools.partial(pair_kernel, plan, len(blocks), sub_tota...  11.8 us
    ppermute x4, starting transfers between devices, per_device(): blocks.append(lax.ppermute(blocks[k], 'rep', [(0, 1), (1, 0)]))  4.26 us
    ppermute x3, starting transfers between devices, per_device(): lax.ppermute(payload, 'box', [(i, i ^ k) for i in range(box_total)])  3.75 us
    ppermute x1, waiting for transfers between devices, per_device(): arrived = lax.ppermute(theirs, 'sub', [(0, 1), (1, 0)])  2.62 us
    unnamed x10, local copies, waits for them, and re-layouts  2.6 us
    ppermute x3, waiting for transfers between devices, per_device(): lax.ppermute(payload, 'box', [(i, i ^ k) for i in range(box_total)])  2.15 us
    pallas_call x1, Pallas kernels, per_device(): pl.pallas_call(functools.partial(pack_kernel, plan), out_shape=[jax.Shape...  1.61 us
    add x1, other arithmetic, per_device(): return (mine + arrived).reshape(1, tiles // 2, 3, LANES)  0.63 us
  transfers between devices with their start and end apart: 8, of which 3 were waited for; matrix products, arithmetic and copies ran while one was open for 0% of the time, Pallas kernels for 1%

commit v1 on v0

--- a/solution.py
+++ b/solution.py
@@ -24,7 +24,9 @@
 SUBLANES = 8
 UNROLL = 4
 PREPARE_VMEM = 16 * 1024 * 1024
+PACK_VMEM = 4 * 1024 * 1024
 PAIR_VMEM = 24 * 1024 * 1024
+LATE_PAIRS = 28
 EXCLUDE = 256.0
 FAR_GROUP = 1048576.0
 
@@ -55,16 +57,17 @@
         self.tile_bits = log2_up(tiles + 1)
         self.tile_pad = 1 << self.tile_bits
         self.home_pad = ceil_div(homes, SUBLANES) * SUBLANES
+        self.list_rows = ceil_div(homes * pairs + 5 * UNROLL, LANES) + 1
 
 
 def pack_kernel(plan, *refs):
-    sources, (out_ref, table, groups), targets, sem = refs[:8], refs[8:11], refs[11:19], refs[19]
+    count_ref, sources, (out_ref, table, groups), targets, sem = refs[0], refs[1:8], refs[8:11], refs[11:18], refs[18]
     copies = [pltpu.make_async_copy(a, b, sem.at[n]) for n, (a, b) in enumerate(zip(sources, targets))]
     for copy in copies:
         copy.start()
     for copy in copies:
         copy.wait()
-    atom_ref, type_ref, info_ref, send_ref, pair_ref, count_ref, rep_ref, disp_ref = targets
+    atom_ref, type_ref, info_ref, send_ref, pair_ref, rep_ref, disp_ref = targets
     lane = lax.broadcasted_iota(jnp.int32, (1, LANES), 1)
     lane4 = lax.broadcasted_iota(jnp.int32, (4, LANES), 1)
     row4 = lax.broadcasted_iota(jnp.int32, (4, LANES), 0)
@@ -172,13 +175,10 @@
             near_ops[tile, :, block * LANES : (block + 1) * LANES] = jnp.concatenate(sets, axis=0).astype(jnp.bfloat16)
 
 
-def pair_kernel(plan, blocks, sub_total, near_ops, groups, lj_table, *refs):
+def pair_kernel(plan, blocks, halves, near_ops, groups, lj_table, *refs):
     payloads, rest = refs[:blocks], refs[blocks:]
-    outs = rest[: 2 if sub_total == 2 else 1]
-    (data, rep_rows, disp_rows, list_vm, list_sm, acc, sem) = rest[
-        len(outs) : len(rest) - 2 * UNROLL
-    ]
-    sides, products = rest[len(rest) - 2 * UNROLL : len(rest) - UNROLL], rest[len(rest) - UNROLL :]
+    (out, early, list_sm, data, rep_rows, disp_rows), rest = rest[:6], rest[6:]
+    sides, products, (list_vm, acc, sem) = rest[:UNROLL], rest[UNROLL : 2 * UNROLL], rest[2 * UNROLL :]
     homes, rows, cap, tiles = plan.homes, plan.rows, plan.capacity, plan.tiles
     replicas = lax.axis_size("rep")
     my_box, my_rep = lax.axis_index("box"), lax.axis_index("rep")
@@ -237,19 +237,34 @@
     ranks = jnp.concatenate([lane_f + float(r * LANES) for r in range(plan.pair_rows)], axis=0)
     limit = jnp.concatenate([counts] * plan.pair_rows, axis=0)
     own = (near_all >= 0.0) & (near_all < float(plan.tile_pad)) & (ranks < limit)
-    flags = jnp.where(own, 1.0, 0.0)
-    list_rows = flags.shape[0]
+    list_rows = own.shape[0]
+    if halves:
+        half = tiles // 2
+        side = lax.axis_index("sub")
+        kept = jnp.where(side == 0, near_all, float(tiles - 1) - near_all) < float(half)
+        segments = [own & jnp.logical_not(kept), own & kept]
+    else:
+        segments = [own]
+    flags = jnp.concatenate([jnp.where(segment, 1.0, 0.0) for segment in segments], axis=0)
+    flag_rows = flags.shape[0]
     upper = lax.broadcasted_iota(jnp.int32, (LANES, LANES), 0) <= lax.broadcasted_iota(jnp.int32, (LANES, LANES), 1)
     upper = jnp.where(upper, 1.0, 0.0).astype(jnp.bfloat16)
     prefix = jnp.dot(flags.astype(jnp.bfloat16), upper, preferred_element_type=jnp.float32)
     totals = jnp.broadcast_to(jnp.sum(flags, axis=1, keepdims=True), flags.shape)
-    below = lax.broadcasted_iota(jnp.int32, (list_rows, list_rows), 0) > lax.broadcasted_iota(
-        jnp.int32, (list_rows, list_rows), 1
+    below = lax.broadcasted_iota(jnp.int32, (flag_rows, flag_rows), 0) > lax.broadcasted_iota(
+        jnp.int32, (flag_rows, flag_rows), 1
     )
     below = jnp.where(below, 1.0, 0.0).astype(jnp.bfloat16)
     before = jnp.dot(below, totals.astype(jnp.bfloat16), preferred_element_type=jnp.float32)
-    places = jnp.where(own, before + prefix - 1.0, -1.0)
+    ranked = before + prefix - 1.0
     pair_total = jnp.sum(flags).astype(jnp.int32)
+    places = jnp.where(segments[0], ranked[0:list_rows, :], -1.0)
+    first_total = pair_total
+    if halves:
+        places = jnp.where(segments[1], ranked[list_rows:, :], places)
+        theirs = jnp.sum(flags[0:list_rows, :]).astype(jnp.int32)
+        first_total = jnp.maximum(theirs, pair_total - LATE_PAIRS)
+    first_total = (first_total + (UNROLL - 1)) // UNROLL * UNROLL
     far_home = jnp.floor((far_all + 0.5) * (1.0 / plan.tile_pad))
     far_in_home = far_all - far_home * float(plan.tile_pad)
     same_f = jnp.where(same_all, 1.0, 0.0)
@@ -265,7 +280,8 @@
                     far_in_home[r : r + 1, :],
                     far_home[r : r + 1, :],
                     same_f[r : r + 1, :],
-                    jnp.zeros((SUBLANES - 4, LANES), jnp.float32),
+                    jnp.ones((1, LANES), jnp.float32),
+                    jnp.zeros((SUBLANES - 5, LANES), jnp.float32),
                 ],
                 axis=0,
             )
@@ -277,19 +293,17 @@
                 (((1,), (1,)), ((), ())),
                 preferred_element_type=jnp.float32,
             )
-        near, tile, home, same = [digits[k : k + 1, :].astype(jnp.int32) for k in range(4)]
-        near = jnp.where(lane_ids[0:1, :] + block * LANES < pair_total, near, tiles)
+        near, tile, home, same, used = [digits[k : k + 1, :].astype(jnp.int32) for k in range(5)]
+        near = jnp.where(used > 0, near, tiles)
         code = ((home * plan.tile_pad + tile) * plan.tile_pad + near) * 2 + same
         list_vm[pl.ds(block, 1), :] = code
         return carry
 
-    lax.fori_loop(0, (pair_total + 3 * UNROLL) // LANES + 1, list_block, 0)
-    list_copy = pltpu.make_async_copy(list_vm, list_sm, sem)
+    lax.fori_loop(0, (pair_total + 4 * UNROLL) // LANES + 1, list_block, 0)
+    list_copy = pltpu.make_async_copy(list_vm, list_sm.at[0 : plan.list_rows], sem)
     list_copy.start()
 
     bring(0, plan.near)
-    for tile in range(tiles + 1):
-        acc[tile] = jnp.zeros((3, SUBLANES, LANES), jnp.float32)
 
     all_rep, all_disp = lj_table[0:SUBLANES, :], lj_table[SUBLANES : 2 * SUBLANES, :]
 
@@ -308,6 +322,37 @@
     else:
         lax.fori_loop(0, homes, look_up, 0)
     list_copy.wait()
+    list_sm[plan.list_rows, 0] = first_total
+    list_sm[plan.list_rows, 1] = jnp.maximum(pair_total - first_total, 0)
+    run_pairs(plan, near_ops, groups, data, rep_rows, disp_rows, list_sm, acc, sides, products, 0, first_total)
+    if halves:
+        side = lax.axis_index("sub")
+        write_forces(acc, out, (side ^ 1) * (tiles // 2), tiles // 2)
+        write_forces(acc, early, side * (tiles // 2), tiles // 2)
+    else:
+        write_forces(acc, out, 0, tiles)
+
+
+def second_kernel(plan, near_ops, groups, early, list_sm, data, rep_rows, disp_rows, *refs):
+    out, acc = refs[2 * UNROLL], refs[-1]
+    sides, products = refs[2 * UNROLL + 1 : 3 * UNROLL + 1], refs[3 * UNROLL + 1 : -1]
+    start, total = list_sm[plan.list_rows, 0], list_sm[plan.list_rows, 1]
+    run_pairs(plan, near_ops, groups, data, rep_rows, disp_rows, list_sm, acc, sides, products, start, total, False)
+    write_forces(acc, out, lax.axis_index("sub") * (plan.tiles // 2), plan.tiles // 2, early)
+
+
+def write_forces(acc, out, first, count, early=None):
+    for t in range(count):
+        for r in range(3):
+            total = jnp.sum(acc[first + t, r], axis=0, keepdims=True)
+            out[3 * t + r] = total if early is None else total + early[3 * t + r]
+
+
+def run_pairs(plan, near_ops, groups, data, rep_rows, disp_rows, list_sm, acc, sides, products, start, total, fill=True):
+    rows, tiles = plan.rows, plan.tiles
+    row_ids = lax.broadcasted_iota(jnp.int32, (SUBLANES, LANES), 0)
+    for tile in range(tiles + 1):
+        acc[tile] = jnp.zeros((3, SUBLANES, LANES), jnp.float32)
 
     def decode(place):
         code = list_sm[place // LANES, place % LANES]
@@ -350,33 +395,22 @@
         for r in range(3):
             acc[near, r] += total[r]
 
-    for k in range(UNROLL):
-        far_side(k, sides[k])
-    for k in range(UNROLL):
-        multiply(k, sides[k], products[k])
-        far_side(UNROLL + k, sides[k])
+    if fill:
+        for k in range(UNROLL):
+            far_side(start + k, sides[k])
+        for k in range(UNROLL):
+            multiply(start + k, sides[k], products[k])
+            far_side(start + UNROLL + k, sides[k])
 
     def some_pairs(step, carry):
-        place = step * UNROLL
+        place = start + step * UNROLL
         for k in range(UNROLL):
             add_forces(place + k, products[k])
             multiply(place + UNROLL + k, sides[k], products[k])
             far_side(place + 2 * UNROLL + k, sides[k])
         return carry
 
-    lax.fori_loop(0, (pair_total + UNROLL - 1) // UNROLL, some_pairs, 0)
-
-    if sub_total == 2:
-        half = tiles // 2
-        side = lax.axis_index("sub")
-        for n in range(2):
-            first = (side ^ n) * half
-            for t in range(half):
-                for r in range(3):
-                    outs[n][3 * t + r] = jnp.sum(acc[first + t, r], axis=0, keepdims=True)
-    else:
-        for t in range(tiles):
-            outs[0][t] = jnp.sum(acc[t], axis=1)
+    lax.fori_loop(0, (total + UNROLL - 1) // UNROLL, some_pairs, 0)
 
 
 def per_device(
@@ -401,22 +435,23 @@
     smem = pl.BlockSpec(memory_space=pltpu.SMEM)
     hbm = pl.BlockSpec(memory_space=pltpu.HBM)
     info = tile_info[0].T
-    raw = (atom_data[0], atom_type[0], info, send_tiles[0].transpose(2, 0, 1), pair_slots[0, 0].T, pair_count)
+    raw = (atom_data[0], atom_type[0], info, send_tiles[0].transpose(2, 0, 1), pair_slots[0, 0].T)
     raw += (lj_repulsion, lj_dispersion)
-    places = (pltpu.VMEM, pltpu.VMEM, pltpu.SMEM, pltpu.VMEM, pltpu.VMEM, pltpu.SMEM, pltpu.SMEM, pltpu.SMEM)
+    places = (pltpu.VMEM, pltpu.VMEM, pltpu.SMEM, pltpu.VMEM, pltpu.VMEM, pltpu.SMEM, pltpu.SMEM)
     payload, lj_table, groups = pl.pallas_call(
         functools.partial(pack_kernel, plan),
         out_shape=[
-            jax.ShapeDtypeStruct((plan.rows, LANES), jnp.float32),
-            jax.ShapeDtypeStruct((2 * SUBLANES, LANES), jnp.float32),
-            jax.ShapeDtypeStruct((tiles + 1, LANES), jnp.float32),
+            pltpu.VMEM((plan.rows, LANES), jnp.float32),
+            pltpu.VMEM((2 * SUBLANES, LANES), jnp.float32),
+            pltpu.VMEM((tiles + 1, LANES), jnp.float32),
         ],
-        in_specs=[hbm] * len(raw),
+        in_specs=[smem] + [hbm] * len(raw),
         out_specs=[vmem] * 3,
         scratch_shapes=[place(array.shape, array.dtype) for place, array in zip(places, raw)]
         + [pltpu.SemaphoreType.DMA((len(raw),))],
+        compiler_params=pltpu.CompilerParams(vmem_limit_bytes=PACK_VMEM),
         name="pack",
-    )(*raw)
+    )(pair_count, *[pltpu.with_memory_space_constraint(array, pltpu.HBM) for array in raw])
     near_ops = pl.pallas_call(
         functools.partial(prepare_kernel, plan),
         out_shape=jax.ShapeDtypeStruct((tiles + 1, 8 * SUBLANES, 7 * LANES), jnp.bfloat16),
@@ -437,35 +472,46 @@
     else:
         blocks = [lax.all_gather(payload, ("box", "rep"), axis=0, tiled=True)]
 
-    if sub_total == 2:
-        outs = [jax.ShapeDtypeStruct((tiles // 2 * 3, 1, LANES), jnp.float32)] * 2
-    else:
-        outs = [jax.ShapeDtypeStruct((tiles, 3, LANES), jnp.float32)]
-    list_rows = ceil_div(homes * pairs + 3 * UNROLL, LANES) + 1
-    results = pl.pallas_call(
-        functools.partial(pair_kernel, plan, len(blocks), sub_total),
-        out_shape=outs,
+    halves = sub_total == 2
+    count = tiles // 2 if halves else tiles
+    forces = jax.ShapeDtypeStruct((count * 3, 1, LANES), jnp.float32)
+    sums = pltpu.VMEM((tiles + 1, 3, SUBLANES, LANES), jnp.float32)
+    buffers = [jax.ShapeDtypeStruct((LANES, 8 * SUBLANES), jnp.bfloat16)] * UNROLL
+    buffers += [jax.ShapeDtypeStruct((LANES, 7 * LANES), jnp.float32)] * UNROLL
+    results, *state = pl.pallas_call(
+        functools.partial(pair_kernel, plan, len(blocks), halves),
+        out_shape=[
+            forces,
+            forces,
+            jax.ShapeDtypeStruct((plan.list_rows + 1, LANES), jnp.int32),
+            jax.ShapeDtypeStruct((homes * plan.rows, LANES), jnp.float32),
+            jax.ShapeDtypeStruct((homes * plan.tile_pad, LANES), jnp.float32),
+            jax.ShapeDtypeStruct((homes * plan.tile_pad, LANES), jnp.float32),
+        ]
+        + buffers,
         in_specs=[vmem] * (3 + len(blocks)),
-        out_specs=[vmem] * len(outs),
-        scratch_shapes=[
-            pltpu.VMEM((homes * plan.rows, LANES), jnp.float32),
-            pltpu.VMEM((homes * plan.tile_pad, LANES), jnp.float32),
-            pltpu.VMEM((homes * plan.tile_pad, LANES), jnp.float32),
-            pltpu.VMEM((list_rows, LANES), jnp.int32),
-            pltpu.SMEM((list_rows, LANES), jnp.int32),
-            pltpu.VMEM((tiles + 1, 3, SUBLANES, LANES), jnp.float32),
-            pltpu.SemaphoreType.DMA,
-        ]
-        + [pltpu.VMEM((LANES, 8 * SUBLANES), jnp.bfloat16)] * UNROLL
-        + [pltpu.VMEM((LANES, 7 * LANES), jnp.float32)] * UNROLL,
+        out_specs=[vmem] * 2 + [smem] + [vmem] * (3 + len(buffers)),
+        scratch_shapes=[pltpu.VMEM((plan.list_rows, LANES), jnp.int32), sums, pltpu.SemaphoreType.DMA],
         compiler_params=pltpu.CompilerParams(vmem_limit_bytes=PAIR_VMEM),
         name="pairs",
     )(*tables, *blocks)
-    if sub_total == 2:
-        mine, theirs = results
-        arrived = lax.ppermute(theirs, "sub", [(0, 1), (1, 0)])
-        return (mine + arrived).reshape(1, tiles // 2, 3, LANES)
-    return lax.psum_scatter(results[0], "sub", scatter_dimension=0, tiled=True)[None]
+    if not halves:
+        results = results.reshape(tiles, 3, LANES)
+        return lax.psum_scatter(results, "sub", scatter_dimension=0, tiled=True)[None]
+    arrived = lax.ppermute(results, "sub", [(0, 1), (1, 0)])
+    first = 7
+    mine, *_ = pl.pallas_call(
+        functools.partial(second_kernel, plan),
+        out_shape=[forces] + buffers,
+        in_specs=[vmem] * 3 + [smem] + [vmem] * (3 + len(buffers)),
+        out_specs=[vmem] * (1 + len(buffers)),
+        input_output_aliases={first + k: 1 + k for k in range(len(buffers))},
+        scratch_shapes=[sums],
+        compiler_params=pltpu.CompilerParams(vmem_limit_bytes=PAIR_VMEM),
+        cost_estimate=pl.CostEstimate(flops=20000000, bytes_accessed=4000000, transcendentals=0),
+        name="second",
+    )(near_ops, groups, *state)
+    return (mine + arrived).reshape(1, count, 3, LANES)
 
 
 def solution(mesh):

time: 31 us -> 26.8 us (0.86)
  local copies, waits for them, and re-layouts: 2.6 us -> 0 us
  waiting for transfers between devices: 4.79 us -> 2.78 us
  Pallas kernels: 13.8 us -> 14.5 us
    ppermute x1, waiting for transfers between devices: 2.62 us -> 0.01 us  [per_device(): arrived = lax.ppermute(results, 'sub', [(0, 1), (1, 0)])]
    unnamed x10 -> x0, local copies, waits for them, and re-layouts: 2.6 us -> none
    ppermute x4, waiting for transfers between devices: 0.01 us -> 0.78 us  [per_device(): blocks.append(lax.ppermute(blocks[k], 'rep', [(0, 1), (1, 0)]))]
    pallas_call x2 -> x3, Pallas kernels: 13.4 us -> 14 us  [the longest x1 9.32 us: per_device(): pl.pallas_call(functools.partial(pair_kernel, plan, len(blocks), halves),...]
  transfers between devices with their start and end apart: 8 -> 8, of which waited for: 3 -> 3; matrix products, arithmetic and copies ran while one was open for 0% -> 0% of each run, Pallas kernels for 1% -> 16%
where the time goes in v1:
time: 26.8 us; the launch traced here: 26.6 us
  Pallas kernels  14.5 us (54%)
  starting transfers between devices  8.03 us (30%)
  waiting for transfers between devices  2.78 us (10%)
  between operations  0.72 us (3%)
  other arithmetic  0.63 us (2%)
    pallas_call x1, Pallas kernels, per_device(): pl.pallas_call(functools.partial(pair_kernel, plan, len(blocks), halves),...  9.32 us
    ppermute x4, starting transfers between devices, per_device(): blocks.append(lax.ppermute(blocks[k], 'rep', [(0, 1), (1, 0)]))  4.21 us
    ppermute x3, starting transfers between devices, per_device(): lax.ppermute(payload, 'box', [(i, i ^ k) for i in range(box_total)])  3.75 us
    pallas_call x1, Pallas kernels, per_device(): pl.pallas_call(functools.partial(second_kernel, plan), out_shape=[forces]...  3.72 us
    ppermute x3, waiting for transfers between devices, per_device(): lax.ppermute(payload, 'box', [(i, i ^ k) for i in range(box_total)])  1.99 us
    pallas_call x1, Pallas kernels, per_device(): pl.pallas_call(functools.partial(pack_kernel, plan), out_shape=[pltpu.VME...  0.99 us
    ppermute x4, waiting for transfers between devices, per_device(): blocks.append(lax.ppermute(blocks[k], 'rep', [(0, 1), (1, 0)]))  0.78 us
    add x1, other arithmetic, per_device(): return (mine + arrived).reshape(1, count, 3, LANES)  0.63 us
  transfers between devices with their start and end apart: 8, of which 3 were waited for; matrix products, arithmetic and copies ran while one was open for 0% of the time, Pallas kernels for 16%

profile of v1, /device:TPU:5, one launch (start us, length us, event | category | flops | bytes accessed | tf_op | source)
XLA Modules:
  0.0 26.6 jit_solution(2192704901124864588)
XLA Ops:
  0.7 1.0 %pack.1 = (f32[128,128]{1,0:T(8,128)S(1)}, f32[16,128]{1,0:T(8,128)S(1)}, f32[25,128]{1,0:T(8,128)S(1)}) custom-call(s32[1,1]{1,0:T(1,128)S(6)} %copy.25.refs_0_, f32[24,4,128]{2,1,0:T(4,128)} %bitcast.12, s32[24,128]{1,0:T(8,128)} %bitcast.13, s32[2,24]{1,0:T(2,128)} %bitcast.16, s32[3,1,8]{2,1,0:T(1,128)} %bitcast.15, s32[2,192]{1,0:T(2,128)} %bitcast.14, ...), custom_call_target="tpu_custom_call" | custom-call | tf_op jit(solution)/shard_map/pack/pallas_call | solution.py:441
  1.6 3.4 %collective-permute-start.2 = (f32[128,128]{1,0:T(8,128)S(1)}, f32[128,128]{1,0:T(8,128)S(1)}, u32[]{:S(2)}, u32[]{:S(2)}) collective-permute-start(f32[128,128]{1,0:T(8,128)S(1)} %get-tuple-element.23.own_ref.refs_0_), channel_id=1, source_target_pairs={{0,12},{4,8},{8,4},{12,0},{1,13},{5,9},{9,5},{13,1},{2,14},{6,10},... | collective-permute-start | bytes 196616 | tf_op jit(solution)/shard_map/ppermute | solution.py:469
  5.0 0.0 collective-permute-start.1
  5.0 0.4 %collective-permute-start = (f32[128,128]{1,0:T(8,128)S(1)}, f32[128,128]{1,0:T(8,128)S(1)}, u32[]{:S(2)}, u32[]{:S(2)}) collective-permute-start(f32[128,128]{1,0:T(8,128)S(1)} %get-tuple-element.23.own_ref.refs_0_), channel_id=1, source_target_pairs={{0,4},{4,0},{8,12},{12,8},{1,5},{5,1},{9,13},{13,9},{2,6},{6,2},{1... | collective-permute-start | bytes 196616 | tf_op jit(solution)/shard_map/ppermute | solution.py:469
  5.4 1.4 %collective-permute-start.3 = (f32[128,128]{1,0:T(8,128)S(1)}, f32[128,128]{1,0:T(8,128)S(1)}, u32[]{:S(2)}, u32[]{:S(2)}) collective-permute-start(f32[128,128]{1,0:T(8,128)S(1)} %get-tuple-element.23.own_ref.refs_0_), channel_id=1, source_target_pairs={{0,1},{1,0},{2,3},{3,2},{4,5},{5,4},{6,7},{7,6},{8,9},{9,8},{10,11... | collective-permute-start | bytes 196616 | tf_op jit(solution)/shard_map/ppermute | solution.py:471
  6.8 0.0 collective-permute-done.2.refs_3_
  6.8 2.1 %collective-permute-start.6 = (f32[128,128]{1,0:T(8,128)S(1)}, f32[128,128]{1,0:T(8,128)S(1)}, u32[]{:S(2)}, u32[]{:S(2)}) collective-permute-start(f32[128,128]{1,0:T(8,128)S(1)} %collective-permute-done.2.refs_3_), channel_id=1, source_target_pairs={{0,1},{1,0},{2,3},{3,2},{4,5},{5,4},{6,7},{7,6},{8,9},{9,8},{10,11... | collective-permute-start | bytes 196616 | tf_op jit(solution)/shard_map/ppermute | solution.py:471
  8.9 2.0 %collective-permute-done.1.refs_2_ = f32[128,128]{1,0:T(8,128)S(1)} collective-permute-done((f32[128,128]{1,0:T(8,128)S(1)}, f32[128,128]{1,0:T(8,128)S(1)}, u32[]{:S(2)}, u32[]{:S(2)}) %collective-permute-start.1) | collective-permute-done | bytes 65568 | tf_op jit(solution)/shard_map/ppermute | solution.py:469
  10.9 0.7 %collective-permute-start.5 = (f32[128,128]{1,0:T(8,128)S(1)}, f32[128,128]{1,0:T(8,128)S(1)}, u32[]{:S(2)}, u32[]{:S(2)}) collective-permute-start(f32[128,128]{1,0:T(8,128)S(1)} %collective-permute-done.1.refs_2_), channel_id=1, source_target_pairs={{0,1},{1,0},{2,3},{3,2},{4,5},{5,4},{6,7},{7,6},{8,9},{9,8},{10,11... | collective-permute-start | bytes 196616 | tf_op jit(solution)/shard_map/ppermute | solution.py:471
  11.6 0.0 collective-permute-done.refs_1_
  11.6 0.0 collective-permute-start.4
  11.6 0.4 %prepare.1.near_ops = bf16[25,64,896]{2,1,0:T(8,128)(2,1)S(1)} custom-call(f32[128,128]{1,0:T(8,128)S(1)} %get-tuple-element.23.own_ref.refs_0_, f32[16,128]{1,0:T(8,128)S(1)} %get-tuple-element.24.table.lj_table, f32[25,128]{1,0:T(8,128)S(1)} %get-tuple-element.25.groups), custom_call_target="tpu_custom_call" | custom-call | flops 4000000 | bytes 4000000 | tf_op jit(solution)/shard_map/prepare/pallas_call | solution.py:455
  12.1 0.0 collective-permute-done.3.refs_4_
  12.1 0.0 collective-permute-done.6.refs_7_
  12.1 0.4 %collective-permute-done.5.refs_6_ = f32[128,128]{1,0:T(8,128)S(1)} collective-permute-done((f32[128,128]{1,0:T(8,128)S(1)}, f32[128,128]{1,0:T(8,128)S(1)}, u32[]{:S(2)}, u32[]{:S(2)}) %collective-permute-start.5) | collective-permute-done | bytes 65568 | tf_op jit(solution)/shard_map/ppermute | solution.py:471
  12.5 0.4 %collective-permute-done.4.refs_5_ = f32[128,128]{1,0:T(8,128)S(1)} collective-permute-done((f32[128,128]{1,0:T(8,128)S(1)}, f32[128,128]{1,0:T(8,128)S(1)}, u32[]{:S(2)}, u32[]{:S(2)}) %collective-permute-start.4) | collective-permute-done | bytes 65568 | tf_op jit(solution)/shard_map/ppermute | solution.py:471
  12.9 9.3 %pairs.1 = (f32[36,1,128]{2,1,0:T(1,128)S(1)}, f32[36,1,128]{2,1,0:T(1,128)S(1)}, s32[15,128]{1,0:T(8,128)S(1)}, f32[1024,128]{1,0:T(8,128)S(1)}, f32[256,128]{1...) custom-call(bf16[25,64,896]{2,1,0:T(8,128)(2,1)S(1)} %prepare.1.near, ...), custom_call_target="tpu_custom_call" | custom-call | tf_op jit(solution)/shard_map/pairs/pallas_call | solution.py:481
  22.2 0.1 collective-permute-start.7
  22.3 3.7 %second.1 = (f32[36,1,128]{2,1,0:T(1,128)S(1)}, bf16[128,64]{1,0:T(8,128)(2,1)S(1)}, bf16[128,64]{1,0:T(8,128)(2,1)S(1)}, bf16[128,64]{1,0:T(8,128)(2,1)S(1)}, b...) custom-call(bf16[25,64,896]{2,1,0:T(8,128)(2,1)S(1)} %prepare.1.near, ...), custom_call_target="tpu_custom_call", output_to_operand_aliasing={{1}: (7, {}), {2}: (8, {}), {3}: (9, {}), {4}: (10, {}), {5... | custom-call | flops 20000000 | bytes 4000000 | tf_op jit(solution)/shard_map/second/pallas_call | solution.py:503
  26.0 0.0 collective-permute-done.7
  26.0 0.6 %add.3 = f32[36,1,128]{2,1,0:T(1,128)} add(f32[36,1,128]{2,1,0:T(1,128)S(1)} %get-tuple-element.39, f32[36,1,128]{2,1,0:T(1,128)S(1)} %collective-permute-done.7) | non-fusion elementwise | flops 4608 | bytes 55296 | tf_op jit(solution)/shard_map/add | solution.py:514
Async XLA Ops:
  1.6 5.1 %collective-permute-start.2 = (f32[128,128]{1,0:T(8,128)S(1)}, f32[128,128]{1,0:T(8,128)S(1)}, u32[]{:S(2)}, u32[]{:S(2)}) collective-permute-start(f32[128,128]{1,0:T(8,128)S(1)} %get-tuple-element.23.own_ref.refs_0_), channel_id=1, source_target_pairs={{0,12},{4,8},{8,4},{12,0},{1,13},{5,9},{9,5},{13,1},{2,14},{6,10},... | collective-permute-start | bytes 196616 | tf_op jit(solution)/shard_map/ppermute | solution.py:469
  5.0 5.8 %collective-permute-start.1 = (f32[128,128]{1,0:T(8,128)S(1)}, f32[128,128]{1,0:T(8,128)S(1)}, u32[]{:S(2)}, u32[]{:S(2)}) collective-permute-start(f32[128,128]{1,0:T(8,128)S(1)} %get-tuple-element.23.own_ref.refs_0_), channel_id=1, source_target_pairs={{0,8},{4,12},{8,0},{12,4},{1,9},{5,13},{9,1},{13,5},{2,10},{6,14},... | collective-permute-start | bytes 196616 | tf_op jit(solution)/shard_map/ppermute | solution.py:469
  5.0 6.6 %collective-permute-start = (f32[128,128]{1,0:T(8,128)S(1)}, f32[128,128]{1,0:T(8,128)S(1)}, u32[]{:S(2)}, u32[]{:S(2)}) collective-permute-start(f32[128,128]{1,0:T(8,128)S(1)} %get-tuple-element.23.own_ref.refs_0_), channel_id=1, source_target_pairs={{0,4},{4,0},{8,12},{12,8},{1,5},{5,1},{9,13},{13,9},{2,6},{6,2},{1... | collective-permute-start | bytes 196616 | tf_op jit(solution)/shard_map/ppermute | solution.py:469
  5.4 6.7 %collective-permute-start.3 = (f32[128,128]{1,0:T(8,128)S(1)}, f32[128,128]{1,0:T(8,128)S(1)}, u32[]{:S(2)}, u32[]{:S(2)}) collective-permute-start(f32[128,128]{1,0:T(8,128)S(1)} %get-tuple-element.23.own_ref.refs_0_), channel_id=1, source_target_pairs={{0,1},{1,0},{2,3},{3,2},{4,5},{5,4},{6,7},{7,6},{8,9},{9,8},{10,11... | collective-permute-start | bytes 196616 | tf_op jit(solution)/shard_map/ppermute | solution.py:471
  6.8 5.3 %collective-permute-start.6 = (f32[128,128]{1,0:T(8,128)S(1)}, f32[128,128]{1,0:T(8,128)S(1)}, u32[]{:S(2)}, u32[]{:S(2)}) collective-permute-start(f32[128,128]{1,0:T(8,128)S(1)} %collective-permute-done.2.refs_3_), channel_id=1, source_target_pairs={{0,1},{1,0},{2,3},{3,2},{4,5},{5,4},{6,7},{7,6},{8,9},{9,8},{10,11... | collective-permute-start | bytes 196616 | tf_op jit(solution)/shard_map/ppermute | solution.py:471
  10.9 1.6 %collective-permute-start.5 = (f32[128,128]{1,0:T(8,128)S(1)}, f32[128,128]{1,0:T(8,128)S(1)}, u32[]{:S(2)}, u32[]{:S(2)}) collective-permute-start(f32[128,128]{1,0:T(8,128)S(1)} %collective-permute-done.1.refs_2_), channel_id=1, source_target_pairs={{0,1},{1,0},{2,3},{3,2},{4,5},{5,4},{6,7},{7,6},{8,9},{9,8},{10,11... | collective-permute-start | bytes 196616 | tf_op jit(solution)/shard_map/ppermute | solution.py:471
  11.6 1.3 %collective-permute-start.4 = (f32[128,128]{1,0:T(8,128)S(1)}, f32[128,128]{1,0:T(8,128)S(1)}, u32[]{:S(2)}, u32[]{:S(2)}) collective-permute-start(f32[128,128]{1,0:T(8,128)S(1)} %collective-permute-done.refs_1_), channel_id=1, source_target_pairs={{0,1},{1,0},{2,3},{3,2},{4,5},{5,4},{6,7},{7,6},{8,9},{9,8},{10,11... | collective-permute-start | bytes 196616 | tf_op jit(solution)/shard_map/ppermute | solution.py:471
  22.2 3.8 %collective-permute-start.7 = (f32[36,1,128]{2,1,0:T(1,128)S(1)}, f32[36,1,128]{2,1,0:T(1,128)S(1)}, u32[]{:S(2)}, u32[]{:S(2)}) collective-permute-start(f32[36,1,128]{2,1,0:T(1,128)S(1)} %get-tuple-element.40), channel_id=1, source_target_pairs={{0,2},{2,0},{1,3},{3,1},{4,6},{6,4},{5,7},{7,5},{8,10},{10,8},{9,1... | collective-permute-start | bytes 55304 | tf_op jit(solution)/shard_map/ppermute | solution.py:501
